TPU v7x, 32 devices: a whole 2x2x4 slice. The times are simulated.
32 devices in a mesh: seq: 16 (over z, x, core), res: 2 (over y).
Axes of the slice: x: 2, y: 2, z: 4, core: 2. Of those that a mesh axis runs over, the one named last changes fastest.
Arguments:
- alignment_rows: bfloat16 [1024, 16, 64], P('seq', 'res'), may hold values from -6 to 6
- pair_features: bfloat16 [16, 16, 128], P('res', 'seq'), may hold values from -6 to 6
- sequence_block_count: int32 [16], P('seq'), may hold values from 16 to 64
- cluster_member_count: int32 [1024], P('seq'), may hold values from 1 to 16
- residue_present_mask: int32 [16], replicated, may hold values 0 or 1
- attention_in_weight: bfloat16 [64, 256], replicated, may hold values from -0.75 to 0.75
- attention_out_weight: bfloat16 [64, 64], replicated, may hold values from -4 to 4
- pair_bias_weight: float32 [128, 8], replicated, may hold values from -48 to 48
- outer_factor_weight: bfloat16 [64, 64], replicated, may hold values from -0.75 to 0.75
- outer_output_weight: float32 [1024, 128], replicated, may hold values from -4 to 4
- outer_product_bias: float32 [128], replicated, may hold values from -3 to 3
Outputs:
- row_attention_update: bfloat16 [1024, 16, 64], P('seq', 'res')
- pair_update: bfloat16 [16, 16, 128], P('seq', 'res')
All inputs are finite; a program needn't handle non-finite values.
Results may differ from a plain program's by a relative error of at most 0.0081.
Values may be sent and summed in bfloat16 or wider, within the bound.
A program may use at most 64 MiB of HBM per device.

v0:
```python
import math

import jax
import jax.numpy as jnp
from jax import lax
from jax.sharding import PartitionSpec as P


def apply_layer_norm(values):
    centre = jnp.mean(values, axis=-1, keepdims=True)
    spread = jnp.mean(jnp.square(values - centre), axis=-1, keepdims=True)
    return (values - centre) * lax.rsqrt(spread + 1e-05)


def apply_row_projection(input_rows, attention_in_weight):
    slot_count, n_res, channel_width = input_rows.shape
    normed_alignment = apply_layer_norm(input_rows.astype(jnp.float32)).astype(jnp.bfloat16)
    projected_rows = jnp.dot(
        normed_alignment.reshape(-1, channel_width),
        attention_in_weight,
        preferred_element_type=jnp.float32,
    ).reshape(slot_count, n_res, 4 * channel_width)
    return projected_rows


def split_projection_parts(projected_rows, head_count):
    channel_width = projected_rows.shape[-1] // 4
    head_dim = channel_width // head_count
    query_rows = (projected_rows[..., :channel_width] * (1.0 / math.sqrt(head_dim))).astype(
        jnp.bfloat16
    )
    key_value_pairs = projected_rows[..., channel_width : 3 * channel_width].astype(jnp.bfloat16)
    gate_activation = jax.nn.sigmoid(projected_rows[..., 3 * channel_width :])
    return (query_rows, key_value_pairs, gate_activation)


def attend(query_rows, key_value_pairs, gate_activation, full_bias, attention_out_weight):
    slot_count, n_query, channel_width = query_rows.shape
    head_count = full_bias.shape[0]
    head_dim = channel_width // head_count
    n_keys = key_value_pairs.shape[1]
    block = math.gcd(slot_count, max(1, (1 << 18) // (head_count * n_query * n_keys)))

    def one_block(pieces):
        query_blk, kv_blk = pieces
        query_heads = query_blk.reshape(block, n_query, head_count, head_dim)
        key_heads = kv_blk[..., :channel_width].reshape(block, n_keys, head_count, head_dim)
        value_heads = kv_blk[..., channel_width:].reshape(block, n_keys, head_count, head_dim)
        scores = (
            jnp.einsum(
                "bihd,bjhd->bhij", query_heads, key_heads, preferred_element_type=jnp.float32
            )
            + full_bias[None]
        )
        row_max = jnp.max(scores, axis=-1, keepdims=True)
        expo = jnp.exp(scores - row_max)
        probs = (expo / jnp.sum(expo, axis=-1, keepdims=True)).astype(jnp.bfloat16)
        context = jnp.einsum(
            "bhij,bjhd->bihd", probs, value_heads, preferred_element_type=jnp.float32
        )
        return context.reshape(block, n_query, channel_width)

    context = lax.map(
        one_block,
        (
            query_rows.reshape(-1, block, n_query, channel_width),
            key_value_pairs.reshape(-1, block, n_keys, 2 * channel_width),
        ),
    )
    context = context.reshape(slot_count, n_query, channel_width)
    gated = (gate_activation * context).astype(jnp.bfloat16)
    update = jnp.dot(
        gated.reshape(-1, channel_width), attention_out_weight, preferred_element_type=jnp.float32
    ).astype(jnp.bfloat16)
    return update.reshape(slot_count, n_query, channel_width)


def local(
    alignment_rows,
    pair_features,
    sequence_block_count,
    cluster_member_count,
    residue_present_mask,
    attention_in_weight,
    attention_out_weight,
    pair_bias_weight,
    outer_factor_weight,
    outer_output_weight,
    outer_product_bias,
):
    slot_count, local_residues, channel_width = alignment_rows.shape
    head_count = pair_bias_weight.shape[1]
    block_length = local_residues * lax.axis_size("res")
    factor_width = outer_factor_weight.shape[1] // 2
    pair_width = outer_output_weight.shape[1]
    usable = (jnp.arange(slot_count, dtype=jnp.int32) < sequence_block_count[0]).astype(jnp.float32)
    seq_weight = cluster_member_count.astype(jnp.float32) * usable
    weight_sum = lax.psum(jnp.sum(seq_weight), "seq")
    key_mask = jnp.where(residue_present_mask == 1, 0.0, -1000000.0).astype(jnp.float32)
    pair_norm = apply_layer_norm(pair_features.astype(jnp.float32))
    bias_tile = jnp.einsum(
        "ijp,ph->hij", pair_norm, pair_bias_weight, precision=lax.Precision.HIGHEST
    )
    bias_local = lax.all_gather(bias_tile, "seq", axis=2, tiled=True) + key_mask[None, None, :]
    query_rows, key_value_pairs, gate_activation = split_projection_parts(
        apply_row_projection(alignment_rows, attention_in_weight), head_count
    )
    keys_all = lax.all_gather(key_value_pairs, "res", axis=1, tiled=True)
    returned = attend(query_rows, keys_all, gate_activation, bias_local, attention_out_weight)
    row_attention_update = returned * usable.astype(jnp.bfloat16)[:, None, None]
    updated_alignment = alignment_rows.astype(jnp.float32) + row_attention_update.astype(
        jnp.float32
    )
    outer_input_norm = apply_layer_norm(updated_alignment).astype(jnp.bfloat16)
    factors = jnp.dot(
        outer_input_norm.reshape(-1, channel_width),
        outer_factor_weight,
        preferred_element_type=jnp.float32,
    ).reshape(slot_count, local_residues, 2 * factor_width)
    res_start = lax.axis_index("res") * local_residues
    res_keep = lax.dynamic_slice_in_dim(residue_present_mask, res_start, local_residues).astype(
        jnp.float32
    )[None, :, None]
    left_proj = (factors[..., :factor_width] * res_keep).astype(jnp.bfloat16)
    right_proj = (factors[..., factor_width:] * res_keep * seq_weight[:, None, None]).astype(
        jnp.bfloat16
    )
    left_all = lax.all_gather(
        left_proj.reshape(slot_count, local_residues * factor_width), "res", axis=1, tiled=True
    )
    left_all = left_all.reshape(slot_count, block_length, factor_width)
    right_flat = right_proj.reshape(slot_count, local_residues * factor_width)
    weight_cube = outer_output_weight.reshape(factor_width, factor_width, pair_width)
    block = math.gcd(block_length // lax.axis_size("seq") * lax.axis_size("seq"), 16)

    def block_term(block_index):
        left_block = lax.dynamic_slice_in_dim(left_all, block_index * block, block, 1)
        outer_block = lax.dot_general(
            left_block.reshape(slot_count, block * factor_width),
            right_flat,
            (((0,), (0,)), ((), ())),
            preferred_element_type=jnp.float32,
        )
        outer_block = outer_block.reshape(block, factor_width, local_residues, factor_width)
        return jnp.einsum(
            "icjd,cdp->ijp", outer_block, weight_cube, precision=lax.Precision.HIGHEST
        )

    blocks_out = lax.map(
        block_term,
        jnp.arange(
            block_length // lax.axis_size("seq") * lax.axis_size("seq") // block, dtype=jnp.int32
        ),
    )
    summed = lax.psum_scatter(
        blocks_out.reshape(
            block_length // lax.axis_size("seq") * lax.axis_size("seq"), local_residues, pair_width
        ),
        "seq",
        scatter_dimension=0,
        tiled=True,
    )
    pair_update = (summed / weight_sum + outer_product_bias).astype(jnp.bfloat16)
    return (row_attention_update, pair_update)


def solution(mesh):
    return jax.shard_map(
        local,
        mesh=mesh,
        in_specs=(
            P("seq", "res", None),
            P("res", "seq", None),
            P("seq"),
            P("seq"),
            P(),
            P(),
            P(),
            P(),
            P(),
            P(),
            P(),
        ),
        out_specs=(P("seq", "res", None), P("seq", "res", None)),
        check_vma=False,
    )
```

profile of v0, /device:TPU:0, one launch (start us, length us, event | category | flops | bytes accessed | tf_op | source)
XLA Modules:
  0.0 156.6 jit_solution(17227083287812688814)
XLA Ops:
  7.2 1.1 convert_reduce_fusion
  8.3 1.1 fusion.14
  9.5 1.2 fusion.24
  10.7 0.1 slice.67
  10.9 7.2 %all_gather.9 = bf16[64,16,128]{2,1,0:T(8,128)(2,1)S(1)} all-gather(bf16[64,8,128]{2,1,0:T(8,128)(2,1)S(1)} %slice.67), channel_id=1, replica_groups=mesh['seq'=16,'res'=2] {'res'}, dimensions={1}, use_global_device_ids=true | all-gather | bytes 393216 | tf_op jit(solution)/shard_map/all_gather | solution.py:108
  18.1 0.1 fusion.58
  18.2 0.5 copy.67
  18.7 0.2 copy.50
  18.9 1.6 %copy.52 = bf16[64,8,8,8]{3,1,2,0:T(8,128)(2,1)S(1)} copy(bf16[64,8,8,8]{0,3,2,1:T(8,128)(2,1)S(1)} %bitcast.71) | data formatting | bytes 131072 | tf_op jit(solution)/shard_map/while/body/eval_jaxpr/reshape | solution.py:46
  20.5 0.1 convert_reduce_fusion.1
  20.6 0.2 fusion.44
  20.8 0.2 convolution_bitcast_fusion.1
  21.1 22.0 %all_gather.10 = f32[8,8,16]{1,0,2:T(8,128)S(1)} all-gather(f32[8,8,1]{1,0,2:T(8,128)S(1)} %bitcast.73), channel_id=1, replica_groups=mesh['seq'=16,'res'=2] {'seq'}, dimensions={2}, use_global_device_ids=true | all-gather | bytes 4352 | tf_op jit(solution)/shard_map/all_gather | solution.py:104
  43.1 0.1 copy.55
  43.2 1.4 copy.66
  44.5 3.0 %fusion.59 = (f32[64,8,8]{2,1,0:T(8,128)}, f32[64,8,8,16]{3,2,1,0:T(8,128)}) fusion(f32[8,8,16]{2,1,0:T(8,128)S(1)} %broadcast_add_fusion, bf16[64,8,8,8]{3,1,2,0:T(8,128)(2,1)S(1)} %copy.52, bf16[64,16,64]{1,2,0:T(8,128)(2,1)S(1)} %copy.67), kind=kOutput, calls=%fused_computation.80 | convolution fusion | flops 1245199 | bytes 479232 | tf_op jit(solution)/shard_map/while/body/eval_jaxpr/sub | solution.py:56
  47.5 2.7 %convolution_bitcast_fusion = f32[64,8,64]{1,2,0:T(8,128)S(1)} fusion(f32[64,8,8,16]{3,2,1,0:T(8,128)} %get-tuple-element.34, bf16[64,16,64]{1,2,0:T(8,128)(2,1)} %copy.66, f32[64,8,8]{2,1,0:T(8,128)} %get-tuple-element.33), kind=kOutput, calls=%fused_computation.7 | convolution fusion | flops 1179648 | bytes 540672 | tf_op jit(solution)/shard_map/while/body/eval_jaxpr/bhij,bjhd->bihd/dot_general | solution.py:58
  50.3 0.6 copy.58
  50.9 1.0 convolution_convert_fusion
  51.9 0.1 copy.59
  52.7 0.2 fusion.23
  53.0 0.2 multiply_reduce_fusion
  53.3 0.2 multiply_convert_fusion
  53.6 0.3 fusion.30
  53.9 5.0 %all_gather.11 = bf16[64,512]{0,1:T(8,128)(2,1)S(1)} all-gather(bf16[64,256]{0,1:T(8,128)(2,1)S(1)} %bitcast.72), channel_id=1, replica_groups=mesh['seq'=16,'res'=2] {'res'}, dimensions={1}, use_global_device_ids=true | all-gather | bytes 98304 | tf_op jit(solution)/shard_map/all_gather | solution.py:128
  58.9 0.7 fusion.57
  59.6 0.5 fusion.36
  60.1 3.5 %fusion.4 = f32[16,8,128]{2,1,0:T(8,128)} fusion(f32[32,32,128,1]{2,1,0,3:T(8,128)S(1)} %bitcast.69, f32[16,32,8,32]{3,1,2,0:T(8,128)S(1)} %fusion.36), kind=kOutput, calls=%fused_computation.9 | convolution fusion | flops 201326592 | bytes 1114112 | tf_op jit(solution)/shard_map/while/body/eval_jaxpr/icjd,cdp->ijp/dot_general | solution.py:145
  63.6 30.0 %psum.7 = f32[]{:T(128)} all-reduce(f32[]{:T(128)} %get-tuple-element.22), channel_id=1, replica_groups=mesh['seq'=16,'res'=2] {'seq'}, use_global_device_ids=true, to_apply=%region_10.11 | all-reduce | flops 1 | bytes 8 | tf_op jit(solution)/shard_map/psum | solution.py:98
  93.7 0.7 dynamic-slice.2
  94.3 52.9 %all-reduce.3.cloned.1.call-done = f32[16,8,128]{2,1,0:T(8,128)} async-done(((f32[16,8,128]{2,1,0:T(8,128)}), f32[16,8,128]{2,1,0:T(8,128)}) %all-reduce.3.cloned.1.call-update) | async-done | bytes 65552
  147.3 2.5 %fusion.48 = bf16[1,8,128]{2,1,0:T(8,128)(2,1)} fusion(f32[16,8,128]{2,1,0:T(8,128)} %all-reduce.3.cloned.1.call-done, u32[]{:T(128)} %bitcast.36, f32[128]{0:T(128)S(1)} %copy-done.6, f32[]{:T(128)} %psum.7), kind=kLoop, calls=%fused_computation.67 | loop fusion | flops 3072 | bytes 6664 | tf_op jit(solution)/shard_map/convert_element_type | solution.py:163
  (37 shorter events, 0.4 us)
Async XLA Ops:
  7.2 53.0 %copy-start = (f32[1024,128]{1,0:T(8,128)S(1)}, f32[1024,128]{1,0:T(8,128)}, u32[]{:S(2)}) copy-start(f32[1024,128]{1,0:T(8,128)} %param.20) | copy-start | bytes 1572868
  7.2 140.1 %all-reduce.3.cloned.1.call-start = ((), (), s32[]{:S(2)}) async-start(), calls=%async_computation | async-start | bytes 131072
  10.9 9.6 %copy-start.4 = (bf16[8,1,128]{2,0,1:T(8,128)(2,1)S(1)}, bf16[8,1,128]{2,0,1:T(8,128)(2,1)}, u32[]{:S(2)}) copy-start(bf16[8,1,128]{2,0,1:T(8,128)(2,1)} %param.12) | copy-start | bytes 6148
  10.9 9.9 %copy-start.7 = (f32[128,8]{0,1:T(8,128)S(1)}, f32[128,8]{0,1:T(8,128)}, u32[]{:S(2)}) copy-start(f32[128,8]{0,1:T(8,128)} %param.18) | copy-start | bytes 12292
  18.1 25.1 %copy-start.8 = (s32[16]{0:T(128)S(1)}, s32[16]{0:T(128)}, u32[]{:S(2)}) copy-start(s32[16]{0:T(128)} %param.15) | copy-start | bytes 196
  50.3 2.4 %copy-start.1 = (bf16[64,8,64]{2,1,0:T(8,128)(2,1)S(1)}, bf16[64,8,64]{2,1,0:T(8,128)(2,1)}, u32[]{:S(2)}) copy-start(bf16[64,8,64]{2,1,0:T(8,128)(2,1)} %param.11) | copy-start | bytes 196612
  50.3 3.2 %copy-start.3 = (bf16[64,64]{1,0:T(8,128)(2,1)S(1)}, bf16[64,64]{1,0:T(8,128)(2,1)}, u32[]{:S(2)}) copy-start(bf16[64,64]{1,0:T(8,128)(2,1)} %param.19) | copy-start | bytes 24580
  50.9 2.6 %copy-start.9 = (s32[16]{0:T(128)S(1)}, s32[16]{0:T(128)}, u32[]{:S(2)}) copy-start(s32[16]{0:T(128)} %param.15) | copy-start | bytes 196
  50.9 8.0 %copy-start.5 = (s32[64]{0:T(128)S(1)}, s32[64]{0:T(128)}, u32[]{:S(2)}) copy-start(s32[64]{0:T(128)} %param.14) | copy-start | bytes 772
  53.0 10.6 %copy-start.2 = (bf16[64,8,64]{2,1,0:T(8,128)(2,1)}, bf16[64,8,64]{2,1,0:T(8,128)(2,1)S(1)}, u32[]{:S(2)}) copy-start(bf16[64,8,64]{2,1,0:T(8,128)(2,1)S(1)} %get-tuple-element.30) | copy-start | bytes 196612
  59.6 34.1 %copy-start.10 = (u32[32]{0:T(128)S(1)}, u32[32]{0:T(128)}, u32[]{:S(2)}) copy-start(u32[32]{0:T(128)} %constant.66) | copy-start | bytes 388
  59.6 87.7 %copy-start.6 = (f32[128]{0:T(128)S(1)}, f32[128]{0:T(128)}, u32[]{:S(2)}) copy-start(f32[128]{0:T(128)} %param.21) | copy-start | bytes 1540
Sparse Core Ops, SparseCore 0:
  63.8 83.4 all-reduce.2
where the time goes:
time: 158 us; the launch traced here: 157 us
  blocking collectives  64.3 us (41%)
  waiting for transfers between devices  53 us (34%)
  between operations  14.9 us (9%)
  matrix products  12.5 us (8%)
  other arithmetic  6.6 us (4%)
  local copies, waits for them, and re-layouts  5.38 us (3%)
    unnamed x2, waiting for transfers between devices  53 us
    psum x1, blocking collectives, local(): weight_sum = lax.psum(jnp.sum(seq_weight), 'seq')  30 us
    all_gather x1, blocking collectives, local(): lax.all_gather(bias_tile, 'seq', axis=2, tiled=True)  22 us
    all_gather x1, blocking collectives, local(): keys_all = lax.all_gather(key_value_pairs, 'res', axis=1, tiled=True)  7.2 us
    all_gather x1, blocking collectives, local(): lax.all_gather(left_proj.reshape(slot_count, local_residues * factor_widt...  5 us
    dot_general x1, matrix products, block_term(): jnp.einsum('icjd,cdp->ijp', outer_block, weight_cube, precision=lax.Preci...  3.48 us
  transfers between devices with their start and end apart: 1, of which 1 were waited for; matrix products, arithmetic and copies ran while one was open for 0% of the time, Pallas kernels for 0%

commit v1 on v0

v1 whole, which is shorter than its diff:
```python
import functools
import math

import jax
import jax.numpy as jnp
from jax import lax
from jax.experimental import pallas as pl
from jax.experimental.pallas import tpu as pltpu
from jax.sharding import PartitionSpec as P

MESH = pl.DeviceIdType.MESH
F32 = jnp.float32
BF16 = jnp.bfloat16
LANES = 128


def dot(a, b, ca, cb, precision=None):
    return lax.dot_general(
        a, b, (((ca,), (cb,)), ((), ())), precision=precision, preferred_element_type=F32
    )


def norm_over(values, axis):
    centre = jnp.mean(values, axis=axis, keepdims=True)
    shifted = values - centre
    spread = jnp.mean(shifted * shifted, axis=axis, keepdims=True)
    return shifted * lax.rsqrt(spread + 1e-05)


def kernel(
    n_seq,
    n_res,
    slots,
    rl,
    heads,
    factor,
    count_ref,
    mask_ref,
    x_ref,
    pair_ref,
    members_ref,
    w_in_ref,
    w_out_ref,
    w_bias_ref,
    w_fac_ref,
    w_proj_hbm,
    bias_ref,
    update_ref,
    pair_out_ref,
    rows32,
    x_t,
    xn_buf,
    xn_recv,
    tile_buf,
    tile_recv,
    q_s,
    kv_s,
    roll_s,
    gate_s,
    bias_s,
    ctx_s,
    left_buf,
    left_recv,
    right_s,
    outer_s,
    w_raw,
    w_perm,
    part_buf,
    part_recv,
    w_sem,
    xn_send_sem,
    xn_recv_sem,
    tile_send_sem,
    tile_recv_sem,
    left_send_sem,
    left_recv_sem,
    part_send_sem,
    part_recv_sem,
):
    me_s = lax.axis_index("seq")
    me_r = lax.axis_index("res")
    width = x_ref.shape[2]
    hd = width // heads
    tiles = rl // 2
    n_keys = rl * n_res
    row_block = n_keys // n_seq
    key_block = pair_ref.shape[0] // rl

    def seq_peer(k):
        return lax.rem(me_s + k, n_seq)

    def res_peer(k):
        return lax.rem(me_r + k, n_res)

    barrier = pltpu.get_barrier_semaphore()

    @pl.loop(1, n_seq)
    def _(k):
        pl.semaphore_signal(barrier, inc=1, device_id=(seq_peer(k), me_r), device_id_type=MESH)

    for k in range(1, n_res):
        pl.semaphore_signal(barrier, inc=1, device_id=(me_s, res_peer(k)), device_id_type=MESH)

    w_copy = pltpu.make_async_copy(w_proj_hbm, w_raw, w_sem)
    w_copy.start()

    lane = lax.broadcasted_iota(jnp.int32, (1, LANES), 1)
    low = lane < slots
    count = count_ref[0]
    usable = (lax.rem(lane, slots) < count).astype(F32)
    members = members_ref[...].astype(F32)
    members = jnp.concatenate([members, members], axis=1)
    seq_weight = members * usable
    own_weight = jnp.sum(jnp.where(low, seq_weight, 0.0), axis=1, keepdims=True)

    pair_norm = norm_over(pair_ref[...].astype(F32), 1)
    pad = jnp.zeros((LANES - pair_norm.shape[0], pair_norm.shape[1]), F32)
    bias_t = dot(
        w_bias_ref[...], jnp.concatenate([pair_norm, pad], axis=0), 0, 1, lax.Precision.HIGHEST
    )
    tile_buf[...] = jnp.where(lane == LANES - 1, own_weight, bias_t)

    rows32[:, :width] = x_ref[...].astype(F32).reshape(slots * rl, width)
    eye = (
        lax.broadcasted_iota(jnp.int32, (width, width), 0)
        == lax.broadcasted_iota(jnp.int32, (width, width), 1)
    ).astype(F32).astype(BF16)
    for t in range(tiles):
        pair_rows = jnp.concatenate(
            [rows32[pl.ds(2 * t + e, slots, stride=rl), :][:, :width] for e in range(2)], axis=0
        ).astype(BF16)
        turned = dot(eye, pair_rows, 1, 1)
        x_t[t] = turned
        xn_buf[t] = norm_over(turned, 0).astype(BF16)

    pl.semaphore_wait(barrier, n_seq - 1 + n_res - 1)

    xn_copies = [
        pltpu.make_async_remote_copy(
            src_ref=xn_buf,
            dst_ref=xn_recv.at[k - 1],
            send_sem=xn_send_sem.at[k - 1],
            recv_sem=xn_recv_sem.at[k - 1],
            device_id=(me_s, res_peer(k)),
            device_id_type=MESH,
        )
        for k in range(1, n_res)
    ]
    for copy in xn_copies:
        copy.start()

    def tile_copy(k):
        return pltpu.make_async_remote_copy(
            src_ref=tile_buf,
            dst_ref=tile_recv.at[me_s],
            send_sem=tile_send_sem.at[k - 1],
            recv_sem=tile_recv_sem.at[k - 1],
            device_id=(seq_peer(k), me_r),
            device_id_type=MESH,
        )

    @pl.loop(1, n_seq)
    def _(k):
        tile_copy(k).start()

    tile_recv[me_s] = tile_buf[...]

    scale = 1.0 / math.sqrt(hd)

    def put_kv(block, t, kv):
        kv = kv.astype(BF16).astype(F32)
        kv_s[block, t] = kv
        roll_s[block, t] = pltpu.roll(kv, slots, 1)

    for t in range(tiles):
        proj = dot(w_in_ref[...], xn_buf[t], 0, 0)
        q_s[t] = (proj[:width] * scale).astype(BF16).astype(F32)
        put_kv(0, t, proj[width : 3 * width])
        gate_s[t] = jax.nn.sigmoid(proj[3 * width :])

    w_copy.wait()
    for d in range(factor):
        w_perm[d * factor : (d + 1) * factor] = w_raw[pl.ds(d, factor, stride=factor), :].astype(BF16)

    @pl.loop(1, n_seq)
    def _(k):
        tile_copy(k).wait()

    weight_sum = jnp.sum(tile_recv[...], axis=0)[:, LANES - 1 : LANES]

    def res_of(block):
        return lax.rem(me_r + n_res - block, n_res)

    for block in range(n_res):
        for u in range(tiles):
            keyed = []
            for e in range(2):
                j = res_of(block) * rl + 2 * u + e
                key_mask = jnp.where(mask_ref[j] == 1, 0.0, -1000000.0).astype(F32)
                tile = tile_recv[j // key_block] + key_mask
                j_in = j % key_block if key_block > 1 else 0
                if key_block > 1:
                    picks = [
                        jnp.sum(
                            jnp.where(lane == i * key_block + j_in, tile, 0.0), axis=1, keepdims=True
                        )
                        for i in range(rl)
                    ]
                else:
                    picks = [tile[:, i : i + 1] for i in range(rl)]
                keyed.append([jnp.broadcast_to(p, (heads, LANES)) for p in picks])
            for t in range(tiles):
                bias_s[t, 0, block, u] = jnp.where(low, keyed[0][2 * t], keyed[1][2 * t + 1])
                bias_s[t, 1, block, u] = jnp.where(low, keyed[1][2 * t], keyed[0][2 * t + 1])

    for block in range(1, n_res):
        xn_copies[block - 1].wait()
        for t in range(tiles):
            put_kv(block, t, dot(w_in_ref[:, width : 3 * width], xn_recv[block - 1, t], 0, 0))

    def heads_of(ref, base, d):
        return ref[pl.ds(base + d, heads, stride=hd), :]

    for t in range(tiles):
        queries = [q_s.at[t][pl.ds(d, heads, stride=hd), :] for d in range(hd)]
        scores = []
        for turn in range(2):
            source = roll_s if turn else kv_s
            for block in range(n_res):
                for u in range(tiles):
                    total = queries[0] * heads_of(source.at[block, u], 0, 0)
                    for d in range(1, hd):
                        total = total + queries[d] * heads_of(source.at[block, u], 0, d)
                    scores.append(total + bias_s[t, turn, block, u])
        top = functools.reduce(jnp.maximum, scores)
        expo = [jnp.exp(s - top) for s in scores]
        norm = 1.0 / functools.reduce(jnp.add, expo)
        probs = [(e * norm).astype(BF16).astype(F32) for e in expo]
        context = [None] * hd
        at = 0
        for turn in range(2):
            source = roll_s if turn else kv_s
            for block in range(n_res):
                for u in range(tiles):
                    for d in range(hd):
                        term = probs[at] * heads_of(source.at[block, u], width, d)
                        context[d] = term if context[d] is None else context[d] + term
                    at += 1
        for d in range(hd):
            ctx_s[t, pl.ds(d, heads, stride=hd), :] = context[d]

    gated_tiles = []
    keep_tiles = []
    for t in range(tiles):
        gated = (gate_s[t] * ctx_s[t]).astype(BF16)
        gated_tiles.append(gated)
        update = dot(w_out_ref[...], gated, 0, 0).astype(BF16).astype(F32) * usable
        outer_norm = norm_over(x_t[t] + update, 0).astype(BF16)
        factors = dot(w_fac_ref[...], outer_norm, 0, 0)
        keeps = [(mask_ref[me_r * rl + 2 * t + e]).astype(F32) for e in range(2)]
        keep = jnp.where(low, keeps[0], keeps[1])
        left_buf[t] = (factors[:factor] * keep).astype(BF16)
        right = factors[factor:] * keep * seq_weight
        turned = pltpu.roll(right, slots, 1)
        zero = jnp.zeros_like(right)
        right_s[0, pl.ds(2 * t, factor, stride=rl), :] = jnp.where(low, right, zero)
        right_s[0, pl.ds(2 * t + 1, factor, stride=rl), :] = jnp.where(low, turned, zero)
        right_s[1, pl.ds(2 * t, factor, stride=rl), :] = jnp.where(low, zero, turned)
        right_s[1, pl.ds(2 * t + 1, factor, stride=rl), :] = jnp.where(low, zero, right)

    left_copies = [
        pltpu.make_async_remote_copy(
            src_ref=left_buf,
            dst_ref=left_recv.at[k - 1],
            send_sem=left_send_sem.at[k - 1],
            recv_sem=left_recv_sem.at[k - 1],
            device_id=(me_s, res_peer(k)),
            device_id_type=MESH,
        )
        for k in range(1, n_res)
    ]
    for copy in left_copies:
        copy.start()

    right_all = right_s[...].reshape(2 * factor * rl, LANES).astype(BF16)
    groups = LANES // factor
    even = lax.rem(lane // factor, 2) == 0

    def project(block, left):
        products = dot(right_all, left.reshape(tiles * factor, LANES), 1, 1)
        for half in range(2):
            for g in range(factor // groups):
                base = (half * factor + g * groups) * rl
                a = [products[base + k * rl : base + (k + 1) * rl] for k in range(groups)]
                p0 = jnp.where(low, a[0], pltpu.roll(a[2], 64, 1))
                p2 = jnp.where(low, pltpu.roll(a[0], 64, 1), a[2])
                p1 = jnp.where(low, a[1], pltpu.roll(a[3], 64, 1))
                p3 = jnp.where(low, pltpu.roll(a[1], 64, 1), a[3])
                out = [
                    jnp.where(even, p0, pltpu.roll(p1, 32, 1)),
                    jnp.where(even, pltpu.roll(p0, 96, 1), p1),
                    jnp.where(even, p2, pltpu.roll(p3, 32, 1)),
                    jnp.where(even, pltpu.roll(p2, 96, 1), p3),
                ]
                for ip in range(groups):
                    i = 2 * ip + half
                    outer_s[i * rl : (i + 1) * rl, g * LANES : (g + 1) * LANES] = out[ip]
        part = dot(outer_s[...].astype(BF16), w_perm[...], 1, 0)
        part_buf[pl.ds(res_of(block) * rl, rl)] = part.reshape(rl, rl, part.shape[1])

    project(0, left_buf[...])

    row = lax.broadcasted_iota(jnp.int32, (slots, 1), 0)
    row_usable = (row < count).astype(F32)
    w_out_wide = jnp.concatenate([w_out_ref[...], w_out_ref[...]], axis=1)
    for t in range(tiles):
        plain = dot(gated_tiles[t], w_out_wide, 0, 0).astype(BF16).astype(F32)
        for e in range(2):
            rows32[pl.ds(2 * t + e, slots, stride=rl), :] = (
                plain[e * slots : (e + 1) * slots] * row_usable
            )
    update_ref[...] = rows32[:, :width].reshape(slots, rl, width).astype(BF16)

    for block in range(1, n_res):
        left_copies[block - 1].wait()
        project(block, left_recv[block - 1])

    def part_copy(k):
        owner = seq_peer(k)
        return pltpu.make_async_remote_copy(
            src_ref=part_buf.at[pl.ds(owner * row_block, row_block)],
            dst_ref=part_recv.at[k - 1],
            send_sem=part_send_sem.at[k - 1],
            recv_sem=part_recv_sem.at[k - 1],
            device_id=(owner, me_r),
            device_id_type=MESH,
        )

    @pl.loop(1, n_seq)
    def _(k):
        part_copy(k).start()

    @pl.loop(1, n_seq)
    def _(k):
        part_copy(k).wait()

    total = part_buf[pl.ds(me_s * row_block, row_block)] + jnp.sum(part_recv[...], axis=0)
    pair_out_ref[...] = (total / weight_sum[None] + bias_ref[...][None]).astype(BF16)


def solution(mesh):
    n_seq = mesh.shape["seq"]
    n_res = mesh.shape["res"]

    def local(
        alignment_rows,
        pair_features,
        sequence_block_count,
        cluster_member_count,
        residue_present_mask,
        attention_in_weight,
        attention_out_weight,
        pair_bias_weight,
        outer_factor_weight,
        outer_output_weight,
        outer_product_bias,
    ):
        slots, rl, width = alignment_rows.shape
        heads = pair_bias_weight.shape[1]
        factor = outer_factor_weight.shape[1] // 2
        pair_width = outer_output_weight.shape[1]
        key_block = pair_features.shape[1]
        row_block = rl * n_res // n_seq
        tiles = rl // 2
        assert 2 * slots == LANES and tiles * factor == LANES and 4 * factor == LANES
        assert pair_width == LANES and heads == 8 and rl == 8
        vmem = pl.BlockSpec(memory_space=pltpu.VMEM)
        smem = pl.BlockSpec(memory_space=pltpu.SMEM)
        dma = pltpu.SemaphoreType.DMA
        return pl.pallas_call(
            functools.partial(kernel, n_seq, n_res, slots, rl, heads, factor),
            out_shape=(
                jax.ShapeDtypeStruct((slots, rl, width), BF16),
                jax.ShapeDtypeStruct((row_block, rl, pair_width), BF16),
            ),
            in_specs=[smem, smem] + [vmem] * 7 + [pl.BlockSpec(memory_space=pl.ANY), vmem],
            out_specs=(vmem, vmem),
            scratch_shapes=[
                pltpu.VMEM((slots * rl, LANES), F32),
                pltpu.VMEM((tiles, width, LANES), F32),
                pltpu.VMEM((tiles, width, LANES), BF16),
                pltpu.VMEM((n_res - 1, tiles, width, LANES), BF16),
                pltpu.VMEM((heads, LANES), F32),
                pltpu.VMEM((n_seq, heads, LANES), F32),
                pltpu.VMEM((tiles, width, LANES), F32),
                pltpu.VMEM((n_res, tiles, 2 * width, LANES), F32),
                pltpu.VMEM((n_res, tiles, 2 * width, LANES), F32),
                pltpu.VMEM((tiles, width, LANES), F32),
                pltpu.VMEM((tiles, 2, n_res, tiles, heads, LANES), F32),
                pltpu.VMEM((tiles, width, LANES), F32),
                pltpu.VMEM((tiles, factor, LANES), BF16),
                pltpu.VMEM((n_res - 1, tiles, factor, LANES), BF16),
                pltpu.VMEM((2, factor * rl, LANES), F32),
                pltpu.VMEM((rl * rl, factor * factor), F32),
                pltpu.VMEM((factor * factor, pair_width), F32),
                pltpu.VMEM((factor * factor, pair_width), BF16),
                pltpu.VMEM((rl * n_res, rl, pair_width), F32),
                pltpu.VMEM((n_seq - 1, row_block, rl, pair_width), F32),
                dma,
                dma((n_res - 1,)),
                dma((n_res - 1,)),
                dma((n_seq - 1,)),
                dma((n_seq - 1,)),
                dma((n_res - 1,)),
                dma((n_res - 1,)),
                dma((n_seq - 1,)),
                dma((n_seq - 1,)),
            ],
            compiler_params=pltpu.CompilerParams(collective_id=0, has_side_effects=True),
        )(
            sequence_block_count,
            residue_present_mask,
            alignment_rows,
            pair_features.reshape(rl * key_block, pair_features.shape[2]),
            cluster_member_count.reshape(1, slots),
            attention_in_weight,
            attention_out_weight,
            pair_bias_weight,
            outer_factor_weight,
            outer_output_weight,
            outer_product_bias.reshape(1, pair_width),
        )

    return jax.shard_map(
        local,
        mesh=mesh,
        in_specs=(
            P("seq", "res", None),
            P("res", "seq", None),
            P("seq"),
            P("seq"),
            P(),
            P(),
            P(),
            P(),
            P(),
            P(),
            P(),
        ),
        out_specs=(P("seq", "res", None), P("seq", "res", None)),
        check_vma=False,
    )
```

time: 158 us -> 26.8 us (0.17)
  blocking collectives: 64.3 us -> 0 us
  waiting for transfers between devices: 53 us -> 0 us
  Pallas kernels: 0 us -> 22.4 us
  between operations: 14.9 us -> 1.31 us
  matrix products: 12.5 us -> 0 us
  other arithmetic: 6.6 us -> 0 us
  local copies, waits for them, and re-layouts: 5.38 us -> 2.9 us
    unnamed x2 -> x0, waiting for transfers between devices: 53 us -> none
    all_gather x3 -> x0, blocking collectives: 34.2 us -> none  [the longest x1 22 us: local(): lax.all_gather(bias_tile, 'seq', axis=2, tiled=True)]
    psum x1 -> x0, blocking collectives: 30 us -> none  [local(): weight_sum = lax.psum(jnp.sum(seq_weight), 'seq')]
    pallas_call x0 -> x1, Pallas kernels: none -> 22.4 us  [local(): pl.pallas_call(functools.partial(kernel, n_seq, n_res, slots, rl, heads,...]
    dot_general x7 -> x0, matrix products: 9.46 us -> none  [the longest x1 3.48 us: block_term(): jnp.einsum('icjd,cdp->ijp', outer_block, weight_cube, precision=lax.Preci...]
    reshape x4 -> x0, local copies, waits for them, and re-layouts: 3.99 us -> none  [the longest x1 1.58 us: one_block(): query_heads = query_blk.reshape(block, n_query, head_count, head_dim)]
    reduce_sum x7 -> x0, other arithmetic: 3.64 us -> none  [the longest x3 1.54 us: apply_layer_norm(): spread = jnp.mean(jnp.square(values - centre), axis=-1, keepdims=True)]
    sub x1 -> x0, matrix products: 3.01 us -> none  [one_block(): expo = jnp.exp(scores - row_max)]
  transfers between devices with their start and end apart: 1 -> 0, of which waited for: 1 -> 0; matrix products, arithmetic and copies ran while one was open for 0% -> 0% of each run, Pallas kernels for 0% -> 0%
where the time goes in v1:
time: 26.8 us; the launch traced here: 26.6 us
  Pallas kernels  22.4 us (84%)
  local copies, waits for them, and re-layouts  2.9 us (11%)
  between operations  1.31 us (5%)
    pallas_call x1, Pallas kernels, local(): pl.pallas_call(functools.partial(kernel, n_seq, n_res, slots, rl, heads,...  22.4 us
    unnamed x7, local copies, waits for them, and re-layouts  2.9 us

profile of v1, /device:TPU:0, one launch (start us, length us, event | category | flops | bytes accessed | tf_op | source)
XLA Modules:
  0.0 26.6 jit_solution(5864649550248580658)
XLA Ops:
  0.6 0.0 copy-start
  1.3 0.0 copy-done
  1.3 0.7 %copy.13.w_bias_ref = f32[128,8]{1,0:T(8,128)} copy(f32[128,8]{0,1:T(8,128)S(1)} %copy-done) | data formatting | bytes 8192 | tf_op args[7]
  2.0 22.4 %shard_map.122 = (bf16[64,8,64]{2,1,0:T(8,128)(2,1)}, bf16[1,8,128]{2,1,0:T(8,128)(2,1)}) custom-call(s32[1]{0:T(128)S(6)} %copy.16.count_ref, s32[16]{0:T(128)} %mask_ref.1, bf16[64,8,64]{2,1,0:T(8,128)(2,1)} %x_ref.1, bf16[8,128]{1,0:T(8,128)(2,1)} %bitcast.3, s32[1,64]{1,0:T(1,128)} %bitcast.4, bf16[64,256]{1,0:T(8,128)(2,1)} %w_in_ref.1, ...), custom_call_target="tpu_custom_call" | custom-call | tf_op jit(solution)/shard_map/pallas_call | solution.py:380
  24.4 0.0 copy-start.1
  24.5 1.6 %copy.17 = bf16[64,8,64]{2,1,0:T(8,128)(2,1)} copy(bf16[64,8,64]{2,1,0:T(8,128)(2,1)} %get-tuple-element.4) | data formatting | bytes 131072
  26.0 0.0 copy-done.1
  26.0 0.6 %copy.18 = bf16[1,8,128]{2,1,0:T(8,128)(2,1)} copy(bf16[1,8,128]{2,1,0:T(8,128)(2,1)S(1)} %copy-done.1) | data formatting | bytes 4096
Async XLA Ops:
  0.6 0.7 %copy-start = (f32[128,8]{0,1:T(8,128)S(1)}, f32[128,8]{0,1:T(8,128)}, u32[]{:S(2)}) copy-start(f32[128,8]{0,1:T(8,128)} %param.18) | copy-start | bytes 12292
  24.4 1.6 %copy-start.1 = (bf16[1,8,128]{2,1,0:T(8,128)(2,1)S(1)}, bf16[1,8,128]{2,1,0:T(8,128)(2,1)}, u32[]{:S(2)}) copy-start(bf16[1,8,128]{2,1,0:T(8,128)(2,1)} %get-tuple-element.5) | copy-start | bytes 6148

commit v2 on v1

--- a/solution.py
+++ b/solution.py
@@ -116,7 +116,7 @@
     pair_norm = norm_over(pair_ref[...].astype(F32), 1)
     pad = jnp.zeros((LANES - pair_norm.shape[0], pair_norm.shape[1]), F32)
     bias_t = dot(
-        w_bias_ref[...], jnp.concatenate([pair_norm, pad], axis=0), 0, 1, lax.Precision.HIGHEST
+        w_bias_ref[...], jnp.concatenate([pair_norm, pad], axis=0), 1, 1, lax.Precision.HIGHEST
     )
     tile_buf[...] = jnp.where(lane == LANES - 1, own_weight, bias_t)
 
@@ -425,7 +425,7 @@
             cluster_member_count.reshape(1, slots),
             attention_in_weight,
             attention_out_weight,
-            pair_bias_weight,
+            pair_bias_weight.T,
             outer_factor_weight,
             outer_output_weight,
             outer_product_bias.reshape(1, pair_width),

time: 26.8 us -> 26 us (0.970)
  local copies, waits for them, and re-layouts: 2.9 us -> 2.15 us
    unnamed x7 -> x4, local copies, waits for them, and re-layouts: 2.9 us -> 2.15 us
where the time goes in v2:
time: 26 us; the launch traced here: 25.8 us
  Pallas kernels  22.4 us (86%)
  local copies, waits for them, and re-layouts  2.15 us (8%)
  between operations  1.3 us (5%)
    pallas_call x1, Pallas kernels, local(): pl.pallas_call(functools.partial(kernel, n_seq, n_res, slots, rl, heads,...  22.4 us
    unnamed x4, local copies, waits for them, and re-layouts  2.15 us

profile of v2, /device:TPU:0, one launch (start us, length us, event | category | flops | bytes accessed | tf_op | source)
XLA Modules:
  0.0 25.8 jit_solution(10083033341592962310)
XLA Ops:
  1.3 22.4 %shard_map.122 = (bf16[64,8,64]{2,1,0:T(8,128)(2,1)}, bf16[1,8,128]{2,1,0:T(8,128)(2,1)}) custom-call(s32[1]{0:T(128)S(6)} %copy.15.count_ref, s32[16]{0:T(128)} %mask_ref.1, bf16[64,8,64]{2,1,0:T(8,128)(2,1)} %x_ref.1, bf16[8,128]{1,0:T(8,128)(2,1)} %bitcast.5, s32[1,64]{1,0:T(1,128)} %bitcast.6, bf16[64,256]{1,0:T(8,128)(2,1)} %w_in_ref.1, ...), custom_call_target="tpu_custom_call" | custom-call | tf_op jit(solution)/shard_map/pallas_call | solution.py:380
  23.7 0.0 copy-start
  23.7 1.6 %copy.16 = bf16[64,8,64]{2,1,0:T(8,128)(2,1)} copy(bf16[64,8,64]{2,1,0:T(8,128)(2,1)} %get-tuple-element.4) | data formatting | bytes 131072
  25.2 0.0 copy-done
  25.2 0.6 %copy.17 = bf16[1,8,128]{2,1,0:T(8,128)(2,1)} copy(bf16[1,8,128]{2,1,0:T(8,128)(2,1)S(1)} %copy-done) | data formatting | bytes 4096
Async XLA Ops:
  23.7 1.6 %copy-start = (bf16[1,8,128]{2,1,0:T(8,128)(2,1)S(1)}, bf16[1,8,128]{2,1,0:T(8,128)(2,1)}, u32[]{:S(2)}) copy-start(bf16[1,8,128]{2,1,0:T(8,128)(2,1)} %get-tuple-element.5) | copy-start | bytes 6148
